TPU v7x, 32 devices: a whole 2x2x4 slice. The times are simulated.
32 devices in a mesh: fsdp: 8 (over z, y), seq: 4 (over x, core).
Axes of the slice: x: 2, y: 2, z: 4, core: 2. Of those that a mesh axis runs over, the one named last changes fastest.
Arguments:
- tokens: bfloat16 [8, 1024, 768], P('fsdp', 'seq'), may hold values from -6 to 6
- condition: bfloat16 [8, 768], P('fsdp'), may hold values from -6 to 6
- ada_weight: bfloat16 [2, 768, 4608], P(None, 'fsdp'), may hold values from -0.21875 to 0.21875
- ada_bias: bfloat16 [2, 4608], P(None, 'fsdp'), may hold values from -3 to 3
- qkv_weight: bfloat16 [2, 768, 2304], P(None, 'fsdp'), may hold values from -0.21875 to 0.21875
- qv_bias: bfloat16 [2, 1536], P(None, 'fsdp'), may hold values from -3 to 3
- out_weight: bfloat16 [2, 768, 768], P(None, 'fsdp'), may hold values from -1.25 to 1.25
- out_bias: bfloat16 [2, 768], P(None, 'fsdp'), may hold values from -3 to 3
- up_weight: bfloat16 [2, 768, 3072], P(None, 'fsdp'), may hold values from -0.21875 to 0.21875
- up_bias: bfloat16 [2, 3072], P(None, 'fsdp'), may hold values from -3 to 3
- down_weight: bfloat16 [2, 3072, 768], P(None, 'fsdp'), may hold values from -0.109375 to 0.109375
- down_bias: bfloat16 [2, 768], P(None, 'fsdp'), may hold values from -3 to 3
- cotangent: bfloat16 [8, 1024, 768], P('fsdp', 'seq'), may hold values from -6 to 6
Outputs:
- block_out: bfloat16 [8, 1024, 768], P('fsdp', 'seq')
- grad_tokens: float32 [8, 1024, 768], P('fsdp', 'seq')
- grad_condition: float32 [8, 768], P('fsdp')
- grad_ada_weight: float32 [2, 768, 4608], P(None, 'fsdp')
- grad_ada_bias: float32 [2, 4608], P(None, 'fsdp')
- grad_qkv_weight: float32 [2, 768, 2304], P(None, 'fsdp')
- grad_qv_bias: float32 [2, 1536], P(None, 'fsdp')
- grad_out_weight: float32 [2, 768, 768], P(None, 'fsdp')
- grad_out_bias: float32 [2, 768], P(None, 'fsdp')
- grad_up_weight: float32 [2, 768, 3072], P(None, 'fsdp')
- grad_up_bias: float32 [2, 3072], P(None, 'fsdp')
- grad_down_weight: float32 [2, 3072, 768], P(None, 'fsdp')
- grad_down_bias: float32 [2, 768], P(None, 'fsdp')
All inputs are finite; a program needn't handle non-finite values.
Results may differ from a plain program's by a relative error of at most 0.017.
The roundings to bfloat16 on the way count: a program that leaves them out, or rounds other values in their place, can miss the bound.
Values may be sent and summed in bfloat16 or wider, within the bound.
A program may use at most 256 MiB of HBM per device.

v0:
```python
import jax
import jax.numpy as jnp
from jax import lax
from jax.sharding import PartitionSpec as P

HEAD_DIM = 64
SCORE_SCALE = HEAD_DIM ** (-0.5)
EPSILON = 1e-06
HIGHEST = lax.Precision.HIGHEST
F32 = jnp.float32
BF16 = jnp.bfloat16


def normalize(values):
    centred = values - jnp.mean(values, axis=-1, keepdims=True)
    inverse = lax.rsqrt(jnp.mean(centred * centred, axis=-1, keepdims=True) + EPSILON)
    return (centred * inverse, inverse)


def norm_back(gradient, normed, inverse):
    return inverse * (
        gradient
        - jnp.mean(gradient, axis=-1, keepdims=True)
        - normed * jnp.mean(gradient * normed, axis=-1, keepdims=True)
    )


def mm(a, b):
    return lax.dot_general(a, b, (((1,), (0,)), ((), ())), preferred_element_type=F32)


def mm_nt(a, b):
    return lax.dot_general(a, b, (((1,), (1,)), ((), ())), preferred_element_type=F32)


def mm_tn(a, b):
    return lax.dot_general(a, b, (((0,), (0,)), ((), ())), preferred_element_type=F32)


def split_heads(rows):
    return rows.reshape(rows.shape[0], -1, HEAD_DIM).transpose(1, 0, 2)


def join_heads(heads):
    return heads.transpose(1, 0, 2).reshape(heads.shape[1], -1)


def attend(q, k, v):
    q, k, v = (split_heads(q), split_heads(k), split_heads(v))
    scores = jnp.einsum("hqd,hkd->hqk", q, k, preferred_element_type=F32) * SCORE_SCALE
    logsum = jnp.log(jnp.sum(jnp.exp(scores), axis=-1, keepdims=True))
    prob = jnp.exp(scores - logsum).astype(BF16)
    out = jnp.einsum("hqk,hkd->hqd", prob, v, preferred_element_type=F32)
    return (join_heads(out).astype(BF16), logsum)


def attend_back(q, k, v, logsum, out_grad):
    q, k, v, out_grad = (split_heads(q), split_heads(k), split_heads(v), split_heads(out_grad))
    scores = jnp.einsum("hqd,hkd->hqk", q, k, preferred_element_type=F32) * SCORE_SCALE
    prob = jnp.exp(scores - logsum)
    dv = jnp.einsum("hqk,hqd->hkd", prob.astype(BF16), out_grad, preferred_element_type=F32)
    dp = jnp.einsum("hqd,hkd->hqk", out_grad, v, preferred_element_type=F32)
    inner = jnp.sum(prob * dp, axis=-1, keepdims=True)
    ds = (prob * (dp - inner)).astype(BF16)
    dq = jnp.einsum("hqk,hkd->hqd", ds, k, preferred_element_type=F32) * SCORE_SCALE
    dk = jnp.einsum("hqk,hqd->hkd", ds, q, preferred_element_type=F32) * SCORE_SCALE
    return [join_heads(t).astype(BF16) for t in (dq, dk, dv)]


def gelu_parts(u):
    c = 0.7978845608028654
    inner = c * (u + 0.044715 * (u * u * u))
    t = jnp.tanh(inner)
    value = 0.5 * u * (1.0 + t)
    slope = 0.5 * (1.0 + t) + 0.5 * u * (1.0 - t * t) * (c * (1.0 + 3.0 * 0.044715 * u * u))
    return (value, slope)


def per_device(
    tokens,
    condition,
    ada_weight,
    ada_bias,
    qkv_weight,
    qv_bias,
    out_weight,
    out_bias,
    up_weight,
    up_bias,
    down_weight,
    down_bias,
    cotangent,
):
    n = lax.axis_size("fsdp")
    ns = lax.axis_size("seq")
    f = lax.axis_index("fsdp")
    s = lax.axis_index("seq")
    layers, rows, width6 = ada_weight.shape
    width = rows * n
    ff = up_weight.shape[2]
    hc = width // ns
    fc = ff // (ns * n)

    def take(x, axis):
        return lax.dynamic_index_in_dim(x, s, axis, keepdims=False)

    def own(x, axis, size):
        return lax.dynamic_slice_in_dim(x, f * size, size, axis)

    w_qkv, w_rest = ([], [])
    for l in range(layers):
        q_part = take(qkv_weight[l].reshape(rows, 3, ns, hc), 2).reshape(rows, 3 * hc)
        u_part = take(up_weight[l].reshape(rows, n, ns, fc), 2).reshape(rows, n * fc)
        d_part = take(down_weight[l].reshape(ns, fc, width), 0)
        w_qkv.append(lax.all_gather(q_part, "fsdp", axis=0, tiled=True))
        rest = jnp.concatenate([u_part, d_part, out_weight[l]], axis=1)
        w_rest.append(lax.all_gather(rest, "fsdp", axis=0, tiled=True))
    fw = n * fc
    cond_float = condition.astype(F32)
    cond_act = jax.nn.silu(cond_float).astype(BF16)
    small = jnp.concatenate(
        [
            ada_bias.reshape(-1),
            qv_bias.reshape(-1),
            out_bias.reshape(-1),
            up_bias.reshape(-1),
            down_bias.reshape(-1),
            cond_act.reshape(-1),
        ]
    )
    small = lax.all_gather(small, "fsdp", axis=0, tiled=False)
    pos = 0

    def unpack(per_layer):
        nonlocal pos
        part = small[:, pos : pos + layers * per_layer].reshape(n, layers, per_layer)
        pos += layers * per_layer
        return part.transpose(1, 0, 2).reshape(layers, n * per_layer)

    ada_b = unpack(ada_bias.shape[1]).astype(F32)
    qv_b = unpack(qv_bias.shape[1]).astype(F32)
    out_b = unpack(out_bias.shape[1]).astype(F32)
    up_b = unpack(up_bias.shape[1]).astype(F32)
    down_b = unpack(down_bias.shape[1]).astype(F32)
    cond_all = small[:, pos:]
    cond_rows = own(cond_all, 1, rows)
    q_b = take(qv_b[:, :width].reshape(layers, ns, hc), 1)
    v_b = take(qv_b[:, width:].reshape(layers, ns, hc), 1)
    qkv_b = jnp.concatenate([q_b, jnp.zeros_like(q_b), v_b], axis=1)
    up_bs = take(up_b.reshape(layers, n, ns, fc), 2).reshape(layers, fw)
    mod_partial = jnp.stack([mm(cond_rows, ada_weight[l]) for l in range(layers)], axis=1)
    mod = lax.psum_scatter(mod_partial, "fsdp", scatter_dimension=0, tiled=True)[0] + ada_b
    hidden = tokens[0].astype(F32)
    saved = []
    for l in range(layers):
        shift_a, scale_a, gate_a, shift_m, scale_m, gate_m = jnp.split(mod[l], 6)
        n_a, r_a = normalize(hidden)
        attn_in = (n_a * (1.0 + scale_a) + shift_a).astype(BF16)
        attn_all = lax.all_gather(attn_in, "seq", axis=0, tiled=True)
        qkv = (mm(attn_all, w_qkv[l]) + qkv_b[l]).astype(BF16)
        q, k, v = (qkv[:, :hc], qkv[:, hc : 2 * hc], qkv[:, 2 * hc :])
        head_out, logsum = attend(q, k, v)
        tok_out = lax.all_to_all(head_out, "seq", split_axis=0, concat_axis=1, tiled=True)
        branch = mm(tok_out, w_rest[l][:, fw + width :]) + out_b[l]
        middle = hidden + gate_a * branch
        n_m, r_m = normalize(middle)
        mlp_in = (n_m * (1.0 + scale_m) + shift_m).astype(BF16)
        mlp_all = lax.all_gather(mlp_in, "seq", axis=0, tiled=True)
        up = mm(mlp_all, w_rest[l][:, :fw]) + up_bs[l]
        act = gelu_parts(up)[0].astype(BF16)
        feed = mm(act, w_rest[l][:, fw : fw + width])
        feed = lax.psum_scatter(feed, "seq", scatter_dimension=0, tiled=True) + down_b[l]
        saved.append(
            (n_a, r_a, attn_all, q, k, v, logsum, tok_out, branch, n_m, r_m, mlp_all, up, act, feed)
        )
        hidden = middle + gate_m * feed
    block_out = hidden.astype(BF16)
    g = cotangent[0].astype(F32)
    d_mods = [None] * layers
    reduced = [None] * layers
    bias_grads = [None] * layers
    for l in reversed(range(layers)):
        shift_a, scale_a, gate_a, shift_m, scale_m, gate_m = jnp.split(mod[l], 6)
        n_a, r_a, attn_all, q, k, v, logsum, tok_out, branch, n_m, r_m, mlp_all, up, act, feed = (
            saved[l]
        )
        g_feed = (gate_m * g).astype(BF16)
        d_gate_m = jnp.sum(g * feed, axis=0)
        g_feed_all = lax.all_gather(g_feed, "seq", axis=0, tiled=True)
        grad_down = mm_tn(act, g_feed_all)
        g_up = (mm_nt(g_feed_all, w_rest[l][:, fw : fw + width]) * gelu_parts(up)[1]).astype(BF16)
        grad_up = mm_tn(mlp_all, g_up)
        g_min = lax.psum_scatter(
            mm_nt(g_up, w_rest[l][:, :fw]), "seq", scatter_dimension=0, tiled=True
        )
        d_scale_m = jnp.sum(g_min * n_m, axis=0)
        d_shift_m = jnp.sum(g_min, axis=0)
        g_mid = g + norm_back(g_min * (1.0 + scale_m), n_m, r_m)
        g_branch = (gate_a * g_mid).astype(BF16)
        d_gate_a = jnp.sum(g_mid * branch, axis=0)
        grad_out = mm_tn(tok_out, g_branch)
        g_o = mm_nt(g_branch, w_rest[l][:, fw + width :]).astype(BF16)
        g_o_heads = lax.all_to_all(g_o, "seq", split_axis=1, concat_axis=0, tiled=True)
        dq, dk, dv = attend_back(q, k, v, logsum, g_o_heads)
        g_qkv = jnp.concatenate([dq, dk, dv], axis=1)
        grad_qkv = mm_tn(attn_all, g_qkv)
        g_ain = lax.psum_scatter(mm_nt(g_qkv, w_qkv[l]), "seq", scatter_dimension=0, tiled=True)
        d_scale_a = jnp.sum(g_ain * n_a, axis=0)
        d_shift_a = jnp.sum(g_ain, axis=0)
        g = g_mid + norm_back(g_ain * (1.0 + scale_a), n_a, r_a)
        d_mods[l] = jnp.concatenate(
            [d_shift_a, d_scale_a, d_gate_a, d_shift_m, d_scale_m, d_gate_m]
        )
        packed = jnp.concatenate([grad_up, grad_down, grad_out, grad_qkv], axis=1).astype(BF16)
        reduced[l] = lax.psum_scatter(packed, "fsdp", scatter_dimension=0, tiled=True)

        def place(x, axis):
            zeros = jnp.zeros(x.shape[:axis] + (ns,) + x.shape[axis + 1 :], F32)
            return lax.dynamic_update_slice_in_dim(zeros, x, s, axis)

        qv_g = place(
            jnp.stack([jnp.sum(dq.astype(F32), axis=0), jnp.sum(dv.astype(F32), axis=0)])[
                :, None, :
            ],
            1,
        )
        up_g = place(jnp.sum(g_up.astype(F32), axis=0).reshape(n, 1, fc), 1)
        bias_grads[l] = jnp.concatenate(
            [
                qv_g.reshape(n, -1),
                jnp.sum(g_branch.astype(F32), axis=0).reshape(n, -1),
                up_g.reshape(n, -1),
                jnp.sum(g_feed.astype(F32), axis=0).reshape(n, -1),
            ],
            axis=1,
        )
    red = jnp.stack(reduced)
    shared = jnp.concatenate([red[:, :, : fw + width], red[:, :, fw + 2 * width :]], axis=2)
    shared = lax.all_gather(shared, "seq", axis=0, tiled=False).astype(F32)
    grad_up = (
        shared[..., :fw]
        .reshape(ns, layers, rows, n, fc)
        .transpose(1, 2, 3, 0, 4)
        .reshape(layers, rows, ff)
    )
    grad_down = shared[..., fw : fw + width].transpose(1, 0, 2, 3).reshape(layers, ns * fc, width)
    grad_qkv = shared[..., fw + width :].reshape(ns, layers, rows, 3, hc).transpose(1, 2, 3, 0, 4)
    grad_qkv = grad_qkv.reshape(layers, rows, 3 * width)
    grad_out = lax.psum(red[:, :, fw + width : fw + 2 * width], "seq").astype(F32)
    bias = lax.psum(jnp.stack(bias_grads), ("fsdp", "seq"))
    bias = lax.dynamic_index_in_dim(bias, f, 1, keepdims=False)
    cuts = [qv_bias.shape[1], out_bias.shape[1], up_bias.shape[1], down_bias.shape[1]]
    grad_bias, at = ([], 0)
    for size in cuts:
        grad_bias.append(bias[:, at : at + size])
        at += size
    d_mod = lax.psum(jnp.stack(d_mods), "seq")
    d_mod_all = lax.all_gather(d_mod, "fsdp", axis=0, tiled=False)
    cond_rows32 = cond_rows.astype(F32)
    grad_ada = jnp.stack(
        [
            lax.dot_general(
                cond_rows32,
                d_mod_all[:, l],
                (((0,), (0,)), ((), ())),
                precision=HIGHEST,
                preferred_element_type=F32,
            )
            for l in range(layers)
        ]
    )
    grad_ada_bias = own(jnp.sum(d_mod_all, axis=0), 1, width6 // n)
    g_cond = sum(
        (
            lax.dot_general(
                d_mod_all[:, l],
                ada_weight[l].astype(F32),
                (((1,), (1,)), ((), ())),
                precision=HIGHEST,
                preferred_element_type=F32,
            )
            for l in range(layers)
        )
    )
    g_cond = lax.all_to_all(g_cond, "fsdp", split_axis=0, concat_axis=1, tiled=True)
    _, silu_back = jax.vjp(jax.nn.silu, cond_float)
    grad_condition = silu_back(g_cond)[0]
    return (
        block_out[None],
        g[None],
        grad_condition,
        grad_ada,
        grad_ada_bias,
        grad_qkv,
        grad_bias[0],
        grad_out,
        grad_bias[1],
        grad_up,
        grad_bias[2],
        grad_down,
        grad_bias[3],
    )


def solution(mesh):
    token = P("fsdp", "seq", None)
    matrix = P(None, "fsdp", None)
    vector = P(None, "fsdp")
    return jax.shard_map(
        per_device,
        mesh=mesh,
        in_specs=(token, P("fsdp", None)) + (matrix, vector) * 5 + (token,),
        out_specs=(token, token, P("fsdp", None)) + (matrix, vector) * 5,
        check_vma=False,
    )
```

profile of v0, /device:TPU:0, one launch (start us, length us, event | category | flops | bytes accessed | tf_op | source)
XLA Modules:
  0.0 1008.6 jit_solution(16156190823706369313)
XLA Ops:
  12.4 32.4 %all-gather.2 = bf16[8,1,3456]{2,1,0:T(2,128)(2,1)S(1)} all-gather(bf16[1,1,3456]{2,1,0:T(2,128)(2,1)S(1)} %reshape.391), channel_id=2, replica_groups=mesh['fsdp'=8,'seq'=4] {'fsdp'}, dimensions={0}, use_global_device_ids=true | all-gather | bytes 62208 | tf_op jit(solution)/shard_map/all_gather | solution.py:131
  50.2 71.0 %all-reduce.6.cloned.1.call-done = f32[8,2,4608]{2,1,0:T(2,128)} async-done(((f32[8,2,4608]{2,1,0:T(2,128)}), f32[8,2,4608]{2,1,0:T(2,128)}) %all-reduce.6.cloned.1.call-update) | async-done | bytes 294928
  135.6 34.4 %all_gather.51 = bf16[768,576]{1,0:T(8,128)(2,1)S(1)} all-gather(bf16[96,576]{1,0:T(8,128)(2,1)S(1)} %copy.123), channel_id=1, replica_groups=mesh['fsdp'=8,'seq'=4] {'fsdp'}, dimensions={0}, use_global_device_ids=true | all-gather | bytes 995328 | tf_op jit(solution)/shard_map/all_gather | solution.py:115
  173.0 6.9 fusion.3
  179.9 5.8 fusion.65
  190.8 6.8 all-to-all-done
  197.6 14.9 %all-gather.15.cloned.1.call-done = bf16[768,2304]{1,0:T(8,128)(2,1)} async-done(((bf16[96,2304]{1,0:T(8,128)(2,1)}), bf16[768,2304]{1,0:T(8,128)(2,1)}) %all-gather.15.cloned.1.call-update) | async-done | bytes 3538960 | tf_op jit(solution)/shard_map/all_gather | solution.py:117
  216.7 18.2 %all-gather.17.cloned.1.call-done = bf16[1024,768]{1,0:T(8,128)(2,1)} async-done(((bf16[256,768]{1,0:T(8,128)(2,1)}), bf16[1024,768]{1,0:T(8,128)(2,1)}) %all-gather.17.cloned.1.call-update) | async-done | bytes 1572880 | tf_op jit(solution)/shard_map/all_gather | solution.py:168
  239.7 5.0 fusion.78
  244.9 37.9 %reduce-scatter.13.cloned.1.call-done = f32[256,768]{1,0:T(8,128)} async-done(((f32[1024,768]{1,0:T(8,128)}), f32[256,768]{1,0:T(8,128)}) %reduce-scatter.13.cloned.1.call-update) | async-done | bytes 786448 | tf_op jit(solution)/shard_map/reduce_scatter | solution.py:172
  289.8 32.9 %all_gather.55 = bf16[768,576]{1,0:T(8,128)(2,1)S(1)} all-gather(bf16[96,576]{1,0:T(8,128)(2,1)S(1)} %copy.129), channel_id=1, replica_groups=mesh['fsdp'=8,'seq'=4] {'fsdp'}, dimensions={0}, use_global_device_ids=true | all-gather | bytes 995328 | tf_op jit(solution)/shard_map/all_gather | solution.py:115
  326.3 6.9 fusion.2
  333.2 5.8 fusion.62
  343.8 28.8 %all-gather.21.cloned.1.call-done = bf16[768,2304]{1,0:T(8,128)(2,1)} async-done(((bf16[96,2304]{1,0:T(8,128)(2,1)}), bf16[768,2304]{1,0:T(8,128)(2,1)}) %all-gather.21.cloned.1.call-update) | async-done | bytes 3538960 | tf_op jit(solution)/shard_map/all_gather | solution.py:117
  377.7 17.5 %all-gather.23.cloned.1.call-done = bf16[1024,768]{1,0:T(8,128)(2,1)} async-done(((bf16[256,768]{1,0:T(8,128)(2,1)}), bf16[1024,768]{1,0:T(8,128)(2,1)}) %all-gather.23.cloned.1.call-update) | async-done | bytes 1572880 | tf_op jit(solution)/shard_map/all_gather | solution.py:168
  395.2 4.8 fusion.73
  400.0 17.0 %all-gather.25.cloned.1.call-done = bf16[1024,768]{1,0:T(8,128)(2,1)} async-done(((bf16[256,768]{1,0:T(8,128)(2,1)}), bf16[1024,768]{1,0:T(8,128)(2,1)}) %all-gather.25.cloned.1.call-update) | async-done | bytes 1572880 | tf_op jit(solution)/shard_map/all_gather | solution.py:189
  417.0 5.6 convert_reduce_fusion
  423.7 4.3 fusion.71
  428.1 6.0 fusion.69
  434.2 31.9 %reduce-scatter.17.cloned.1.call-done = f32[256,768]{1,0:T(8,128)} async-done(((f32[1024,768]{1,0:T(8,128)}), f32[256,768]{1,0:T(8,128)}) %reduce-scatter.17.cloned.1.call-update) | async-done | bytes 786448 | tf_op jit(solution)/shard_map/reduce_scatter | solution.py:193
  467.6 38.9 %reduce-scatter.15.cloned.1.call-done = f32[256,768]{1,0:T(8,128)} async-done(((f32[1024,768]{1,0:T(8,128)}), f32[256,768]{1,0:T(8,128)}) %reduce-scatter.15.cloned.1.call-update) | async-done | bytes 786448 | tf_op jit(solution)/shard_map/reduce_scatter | solution.py:172
  511.5 10.2 %all_to_all.80 = bf16[256,4,192]{0,2,1:T(8,128)(2,1)S(1)} all-to-all(bf16[256,4,192]{0,2,1:T(8,128)(2,1)S(1)} %bitcast.284), channel_id=1, replica_groups=mesh['fsdp'=8,'seq'=4] {'seq'}, dimensions={1} | all-to-all | bytes 786432 | tf_op jit(solution)/shard_map/all_to_all | solution.py:203
  523.1 7.5 convert_reduce_fusion.5
  530.6 6.8 multiply_reduce_fusion.1
  537.9 5.2 multiply_convert_fusion.1
  543.1 5.0 fusion.46
  553.4 38.0 %reduce-scatter.19.cloned.1.call-done = f32[256,768]{1,0:T(8,128)} async-done(((f32[1024,768]{1,0:T(8,128)}), f32[256,768]{1,0:T(8,128)}) %reduce-scatter.19.cloned.1.call-update) | async-done | bytes 786448 | tf_op jit(solution)/shard_map/reduce_scatter | solution.py:207
  595.5 19.6 %all-gather.27.cloned.1.call-done = bf16[1024,768]{1,0:T(8,128)(2,1)} async-done(((bf16[256,768]{1,0:T(8,128)(2,1)}), bf16[1024,768]{1,0:T(8,128)(2,1)}) %all-gather.27.cloned.1.call-update) | async-done | bytes 1572880 | tf_op jit(solution)/shard_map/all_gather | solution.py:189
  615.1 5.6 convert_reduce_fusion.1
  621.8 4.3 fusion.80
  636.6 6.5 copy.160
  643.2 21.0 %reduce-scatter.21.cloned.1.call-done = f32[256,768]{1,0:T(8,128)} async-done(((f32[1024,768]{1,0:T(8,128)}), f32[256,768]{1,0:T(8,128)}) %reduce-scatter.21.cloned.1.call-update) | async-done | bytes 786448 | tf_op jit(solution)/shard_map/reduce_scatter | solution.py:193
  670.2 10.0 all_to_all.81
  680.8 11.1 %multiply_reduce_fusion = (f32[3,1024]{1,0:T(4,128)S(1)}, f32[3,1024,1024]{1,2,0:T(8,128)}) fusion(f32[3,1024,1024]{1,2,0:T(8,128)} %fusion.3, bf16[3,1024,64]{1,2,0:T(8,128)(2,1)S(1)} %bitcast.272, bf16[1024,3,64]{0,2,1:T(8,128)(2,1)S(1)} %reshape.363), kind=kOutput, calls=%fused_computation.7 | convolution fusion | flops 408941568 | bytes 25964544 | tf_op jit(solution)/shard_map/hqd,hkd->hqk/dot_general | solution.py:62
  691.9 10.3 %multiply_convert_fusion = bf16[3,1024,1024]{1,2,0:T(8,128)(2,1)S(1)} fusion(f32[3,1024,1024]{1,2,0:T(8,128)} %fusion.3, f32[3,1024,1024]{1,2,0:T(8,128)} %get-tuple-element.173, f32[3,1024]{1,0:T(4,128)S(1)} %get-tuple-element.172), kind=kLoop, calls=%fused_computation.6 | loop fusion | flops 9437184 | bytes 31469568 | tf_op jit(solution)/shard_map/convert_element_type | solution.py:64
  711.4 3.5 convolution_convert_fusion.5
  720.9 6.5 copy.158
  728.6 32.6 %reduce-scatter.27.cloned.1.call-done = bf16[96,2880]{1,0:T(8,128)(2,1)} async-done(((bf16[768,2880]{1,0:T(8,128)(2,1)}), bf16[96,2880]{1,0:T(8,128)(2,1)}) %reduce-scatter.27.cloned.1.call-update) | async-done | bytes 552976
  763.2 40.9 %psum.22 = f32[2,8,768]{2,0,1:T(2,128)S(1)} all-reduce(f32[2,8,768]{2,0,1:T(2,128)S(1)} %pad_maximum_fusion.14), channel_id=1, replica_groups=mesh['fsdp'=8,'seq'=4] {'fsdp','seq'}, use_global_device_ids=true, to_apply=%region_53.54 | all-reduce | flops 12288 | bytes 98304 | tf_op jit(solution)/shard_map/psum | solution.py:250
  807.6 92.1 %reduce-scatter.25.cloned.1.call-done = bf16[96,2880]{1,0:T(8,128)(2,1)} async-done(((bf16[768,2880]{1,0:T(8,128)(2,1)}), bf16[96,2880]{1,0:T(8,128)(2,1)}) %reduce-scatter.25.cloned.1.call-update) | async-done | bytes 552976
  908.4 11.1 %psum.21 = f32[1,2,4608]{2,1,0:T(2,128)S(1)} all-reduce(f32[1,2,4608]{2,1,0:T(2,128)S(1)} %maximum_bitcast_fusion), channel_id=1, replica_groups=mesh['fsdp'=8,'seq'=4] {'seq'}, use_global_device_ids=true, to_apply=%region_39.40 | all-reduce | flops 9216 | bytes 73728 | tf_op jit(solution)/shard_map/psum | solution.py:257
  919.5 31.0 %all_gather.61 = f32[8,2,4608]{2,1,0:T(2,128)S(1)} all-gather(f32[1,2,4608]{2,1,0:T(2,128)S(1)} %psum.21), channel_id=1, replica_groups=mesh['fsdp'=8,'seq'=4] {'fsdp'}, dimensions={0}, use_global_device_ids=true | all-gather | bytes 331776 | tf_op jit(solution)/shard_map/all_gather | solution.py:258
  953.1 5.2 all-to-all-start.4
  968.5 6.8 copy.145
  978.6 5.1 slice_bitcast_fusion
  990.2 5.3 reshape.377
  998.2 3.7 reshape.365
  (399 shorter events, 154.6 us)
Async XLA Ops:
  7.2 42.1 %copy-start.56 = (u32[32]{0:T(128)S(1)}, u32[32]{0:T(128)}, u32[]{:S(2)}) copy-start(u32[32]{0:T(128)} %constant.102) | copy-start | bytes 388
  7.2 41.7 %copy-start.3 = (bf16[1,256,768]{2,1,0:T(8,128)(2,1)S(1)}, bf16[1,256,768]{2,1,0:T(8,128)(2,1)}, u32[]{:S(2)}) copy-start(bf16[1,256,768]{2,1,0:T(8,128)(2,1)} %param.13) | copy-start | bytes 1179652
  7.2 113.9 %all-reduce.6.cloned.1.call-start = ((), (), s32[]{:S(2)}) async-start(), calls=%async_computation.31 | async-start | bytes 589824
  44.8 79.0 %copy-start.29 = (bf16[2,96,3072]{2,1,0:T(8,128)(2,1)S(1)}, bf16[2,96,3072]{2,1,0:T(8,128)(2,1)}, u32[]{:S(2)}) copy-start(bf16[2,96,3072]{2,1,0:T(8,128)(2,1)} %param.21) | copy-start | bytes 3538948
  44.9 76.3 %copy-start.44 = (bf16[8,768]{1,0:T(8,128)(2,1)}, bf16[8,768]{1,0:T(8,128)(2,1)S(1)}, u32[]{:S(2)}) copy-start(bf16[8,768]{1,0:T(8,128)(2,1)S(1)} %get-tuple-element.163) | copy-start | bytes 36868
  48.8 121.1 %all-gather.13.cloned.1.call-start = ((), (), s32[]{:S(2)}) async-start(), calls=%async_computation.13 | async-start | bytes 1966080 | tf_op jit(solution)/shard_map/all_gather | solution.py:159
  49.1 76.8 %copy-start.45 = (f32[256]{0:T(256)}, f32[256]{0:T(256)S(1)}, u32[]{:S(2)}) copy-start(f32[256]{0:T(256)S(1)} %broadcast_multiply_fusion.11) | copy-start | bytes 3076
  50.1 78.1 %copy-start.47 = (f32[256]{0:T(256)}, f32[256]{0:T(256)S(1)}, u32[]{:S(2)}) copy-start(f32[256]{0:T(256)S(1)} %add_rsqrt_fusion.3) | copy-start | bytes 3076
  123.7 88.8 %all-gather.15.cloned.1.call-start = ((), (), s32[]{:S(2)}) async-start(), calls=%async_computation.14 | async-start | bytes 3981312 | tf_op jit(solution)/shard_map/all_gather | solution.py:117
  186.8 10.8 %all-to-all-start = ((bf16[4,256,192]{1,2,0:T(8,128)(2,1)}), bf16[4,256,192]{1,2,0:T(8,128)(2,1)S(1)}, u32[]{:S(2)}, u32[]{:S(2)}) async-start(bf16[4,256,192]{1,2,0:T(8,128)(2,1)} %copy.126), calls=%async_computation | async-start | bytes 786432 | tf_op jit(solution)/shard_map/all_to_all | solution.py:163
  190.2 44.7 %all-gather.17.cloned.1.call-start = ((), (), s32[]{:S(2)}) async-start(), calls=%async_computation.15 | async-start | bytes 1966080 | tf_op jit(solution)/shard_map/all_gather | solution.py:168
  197.6 40.5 %copy-start.13 = (bf16[4,256,192]{1,2,0:T(8,128)(2,1)}, bf16[4,256,192]{1,2,0:T(8,128)(2,1)S(1)}, u32[]{:S(2)}) copy-start(bf16[4,256,192]{1,2,0:T(8,128)(2,1)S(1)} %all-to-all-done) | copy-start | bytes 1179652
  215.2 67.6 %copy-start.1 = (f32[256,768]{1,0:T(8,128)}, f32[256,768]{1,0:T(8,128)S(1)}, u32[]{:S(2)}) copy-start(f32[256,768]{1,0:T(8,128)S(1)} %get-tuple-element.130) | copy-start | bytes 2359300
  216.4 66.4 %reduce-scatter.13.cloned.1.call-start = ((), (), s32[]{:S(2)}) async-start(), calls=%async_computation.16 | async-start | bytes 3932160 | tf_op jit(solution)/shard_map/reduce_scatter | solution.py:172
  244.8 77.9 %all-gather.19.cloned.1.call-start = ((), (), s32[]{:S(2)}) async-start(), calls=%async_computation.17 | async-start | bytes 1966080 | tf_op jit(solution)/shard_map/all_gather | solution.py:159
  285.4 87.2 %all-gather.21.cloned.1.call-start = ((), (), s32[]{:S(2)}) async-start(), calls=%async_computation.18 | async-start | bytes 3981312 | tf_op jit(solution)/shard_map/all_gather | solution.py:117
  326.2 6.9 copy-start.21
  340.0 32.6 %all-to-all-start.1 = ((bf16[4,256,192]{1,2,0:T(8,128)(2,1)}), bf16[4,256,192]{1,2,0:T(8,128)(2,1)S(1)}, u32[]{:S(2)}, u32[]{:S(2)}) async-start(bf16[4,256,192]{1,2,0:T(8,128)(2,1)} %copy.131), calls=%async_computation.2 | async-start | bytes 786432 | tf_op jit(solution)/shard_map/all_to_all | solution.py:163
  343.5 51.7 %all-gather.23.cloned.1.call-start = ((), (), s32[]{:S(2)}) async-start(), calls=%async_computation.19 | async-start | bytes 1966080 | tf_op jit(solution)/shard_map/all_gather | solution.py:168
  376.7 40.3 %all-gather.25.cloned.1.call-start = ((), (), s32[]{:S(2)}) async-start(), calls=%async_computation.21 | async-start | bytes 1966080 | tf_op jit(solution)/shard_map/all_gather | solution.py:189
  377.6 88.5 %reduce-scatter.17.cloned.1.call-start = ((), (), s32[]{:S(2)}) async-start(), calls=%async_computation.22 | async-start | bytes 3932160 | tf_op jit(solution)/shard_map/reduce_scatter | solution.py:193
  428.0 78.5 %reduce-scatter.15.cloned.1.call-start = ((), (), s32[]{:S(2)}) async-start(), calls=%async_computation.20 | async-start | bytes 3932160 | tf_op jit(solution)/shard_map/reduce_scatter | solution.py:172
  434.1 157.3 %reduce-scatter.19.cloned.1.call-start = ((), (), s32[]{:S(2)}) async-start(), calls=%async_computation.23 | async-start | bytes 3932160 | tf_op jit(solution)/shard_map/reduce_scatter | solution.py:207
  509.4 12.3 %copy-start.23 = (bf16[256,768]{1,0:T(8,128)(2,1)}, bf16[256,768]{1,0:T(8,128)(2,1)S(1)}, u32[]{:S(2)}) copy-start(bf16[256,768]{1,0:T(8,128)(2,1)S(1)} %get-tuple-element.150) | copy-start | bytes 1179652
  523.1 14.3 %slice-start.3 = ((s8[12582912]{0:T(1024)(128)(4,1)}), s8[4194304]{0:T(1024)(128)(4,1)S(1)}, s32[]{:S(2)}) async-start(s8[12582912]{0:T(1024)(128)(4,1)} %bitcast.259), calls=%async_computation.35 | async-start | bytes 8388608
  530.6 7.3 slice-start.5
  553.3 39.6 %copy-start.15 = (f32[256,768]{1,0:T(8,128)S(1)}, f32[256,768]{1,0:T(8,128)}, u32[]{:S(2)}) copy-start(f32[256,768]{1,0:T(8,128)} %get-tuple-element.151) | copy-start | bytes 2359300
  553.3 39.6 %copy-start.16 = (f32[256,768]{1,0:T(8,128)S(1)}, f32[256,768]{1,0:T(8,128)}, u32[]{:S(2)}) copy-start(f32[256,768]{1,0:T(8,128)} %get-tuple-element.169) | copy-start | bytes 2359300
  553.4 61.7 %all-gather.27.cloned.1.call-start = ((), (), s32[]{:S(2)}) async-start(), calls=%async_computation.24 | async-start | bytes 1966080 | tf_op jit(solution)/shard_map/all_gather | solution.py:189
  595.3 68.9 %reduce-scatter.21.cloned.1.call-start = ((), (), s32[]{:S(2)}) async-start(), calls=%async_computation.25 | async-start | bytes 3932160 | tf_op jit(solution)/shard_map/reduce_scatter | solution.py:193
  626.2 135.1 %reduce-scatter.27.cloned.1.call-start = ((), (), s32[]{:S(2)}) async-start(), calls=%async_computation.30 | async-start | bytes 5087232
  643.1 21.1 %copy-start.2 = (f32[256,768]{1,0:T(8,128)S(1)}, f32[256,768]{1,0:T(8,128)}, u32[]{:S(2)}) copy-start(f32[256,768]{1,0:T(8,128)} %copy-done.1) | copy-start | bytes 2359300
  643.1 22.6 %copy-start.18 = (f32[256,768]{1,0:T(8,128)S(1)}, f32[256,768]{1,0:T(8,128)}, u32[]{:S(2)}) copy-start(f32[256,768]{1,0:T(8,128)} %reduce-scatter.13.cloned.1.call-done) | copy-start | bytes 2359300
  643.2 162.8 %reduce-scatter.23.cloned.1.call-start = ((), (), s32[]{:S(2)}) async-start(), calls=%async_computation.26 | async-start | bytes 3932160 | tf_op jit(solution)/shard_map/reduce_scatter | solution.py:207
  668.2 12.6 %copy-start.8 = (bf16[1024,192]{0,1:T(8,128)(2,1)S(1)}, bf16[1024,192]{0,1:T(8,128)(2,1)}, u32[]{:S(2)}) copy-start(bf16[1024,192]{0,1:T(8,128)(2,1)} %copy-done.7) | copy-start | bytes 1179652
  680.8 24.8 %slice-start = ((s8[12582912]{0:T(1024)(128)(4,1)}), s8[4194304]{0:T(1024)(128)(4,1)S(1)}, s32[]{:S(2)}) async-start(s8[12582912]{0:T(1024)(128)(4,1)} %bitcast.257), calls=%async_computation.32 | async-start | bytes 8388608
  680.8 24.8 %slice-start.1 = ((s8[12582912]{0:T(1024)(128)(4,1)}), s8[4194304]{0:T(1024)(128)(4,1)S(1)}, s32[]{:S(2)}) async-start(s8[12582912]{0:T(1024)(128)(4,1)} %bitcast.257), calls=%async_computation.33 | async-start | bytes 8388608
  691.9 10.3 %copy-start.26 = (bf16[1024,192]{0,1:T(8,128)(2,1)S(1)}, bf16[1024,192]{0,1:T(8,128)(2,1)}, u32[]{:S(2)}) copy-start(bf16[1024,192]{0,1:T(8,128)(2,1)} %copy-done.25) | copy-start | bytes 1179652
  691.9 13.7 %slice-start.2 = ((s8[12582912]{0:T(1024)(128)(4,1)}), s8[4194304]{0:T(1024)(128)(4,1)S(1)}, s32[]{:S(2)}) async-start(s8[12582912]{0:T(1024)(128)(4,1)} %bitcast.257), calls=%async_computation.34 | async-start | bytes 8388608
  710.9 188.8 %reduce-scatter.25.cloned.1.call-start = ((), (), s32[]{:S(2)}) async-start(), calls=%async_computation.29 | async-start | bytes 5087232
  727.4 78.6 %copy-start.4 = (bf16[1,256,768]{2,1,0:T(8,128)(2,1)S(1)}, bf16[1,256,768]{2,1,0:T(8,128)(2,1)}, u32[]{:S(2)}) copy-start(bf16[1,256,768]{2,1,0:T(8,128)(2,1)} %param.13) | copy-start | bytes 1179652
  727.4 78.6 %copy-start.43 = (f32[768]{0:T(1024)S(1)}, f32[768]{0:T(1024)}, u32[]{:S(2)}) copy-start(f32[768]{0:T(1024)} %copy-done.42) | copy-start | bytes 9220
  727.4 78.6 %copy-start.46 = (f32[256]{0:T(256)S(1)}, f32[256]{0:T(256)}, u32[]{:S(2)}) copy-start(f32[256]{0:T(256)} %copy-done.45) | copy-start | bytes 3076
  727.4 78.6 %copy-start.48 = (f32[256]{0:T(256)S(1)}, f32[256]{0:T(256)}, u32[]{:S(2)}) copy-start(f32[256]{0:T(256)} %copy-done.47) | copy-start | bytes 3076
  727.4 239.0 %all-reduce.4.cloned.1.call-start = ((), (), s32[]{:S(2)}) async-start(), calls=%async_computation.27 | async-start | bytes 786432 | tf_op jit(solution)/shard_map/psum | solution.py:249
  902.9 65.5 %all-gather.29.cloned.1.call-start = ((), (), s32[]{:S(2)}) async-start(), calls=%async_computation.28 | async-start | bytes 4177920 | tf_op jit(solution)/shard_map/all_gather | solution.py:239
  905.5 45.3 %copy-start.6 = (bf16[2,96,4608]{2,1,0:T(8,128)(2,1)S(1)}, bf16[2,96,4608]{2,1,0:T(8,128)(2,1)}, u32[]{:S(2)}) copy-start(bf16[2,96,4608]{2,1,0:T(8,128)(2,1)} %param.15) | copy-start | bytes 5308420
  953.1 11.6 %all-to-all-start.4 = ((f32[8,1,96]{2,1,0:T(1,128)}), f32[8,1,96]{2,1,0:T(1,128)S(1)}, u32[]{:S(2)}, u32[]{:S(2)}) async-start(f32[8,1,96]{2,1,0:T(1,128)} %bitcast.68), calls=%async_computation.10 | async-start | bytes 8192 | tf_op jit(solution)/shard_map/all_to_all | solution.py:285
  (42 other events, 143.0 us)
Sparse Core Ops, SparseCore 0:
  49.0 72.1 all-reduce.5
  123.8 18.6 all-gather.12
  145.3 67.1 all-gather.14
  216.5 18.3 all-gather.16
  244.9 37.8 reduce-scatter.12
  285.5 19.6 all-gather.18
  307.9 64.5 all-gather.20
  376.8 18.3 all-gather.22
  397.3 19.6 all-gather.24
  428.2 37.8 reduce-scatter.16
  468.6 37.8 reduce-scatter.14
  553.5 37.8 reduce-scatter.18
  595.4 19.6 all-gather.26
  626.3 37.8 reduce-scatter.20
  667.7 93.5 reduce-scatter.26
  764.2 37.6 reduce-scatter.22
  805.4 94.2 reduce-scatter.24
  903.1 32.5 all-reduce.3
  937.8 29.6 all-gather.28
where the time goes:
time: 1020 us; the launch traced here: 1010 us
  waiting for transfers between devices  487 us (48%)
  blocking collectives  203 us (20%)
  matrix products  144 us (14%)
  local copies, waits for them, and re-layouts  90.3 us (9%)
  other arithmetic  55.2 us (5%)
  between operations  15.6 us (2%)
  starting transfers between devices  13.8 us (1%)
    unnamed x22, waiting for transfers between devices  196 us
    reduce_scatter x2, waiting for transfers between devices, per_device(): lax.psum_scatter(feed, 'seq', scatter_dimension=0, tiled=True) + down_b[l]  76.8 us
    all_gather x2, blocking collectives, per_device(): w_qkv.append(lax.all_gather(q_part, 'fsdp', axis=0, tiled=True))  67.3 us
    reduce_scatter x2, waiting for transfers between devices, per_device(): lax.psum_scatter(mm_nt(g_up, w_rest[l][:, :fw]), 'seq', scatter_dimension...  52.9 us
    all_gather x2, waiting for transfers between devices, per_device(): w_rest.append(lax.all_gather(rest, 'fsdp', axis=0, tiled=True))  43.6 us
    psum x1, blocking collectives, per_device(): bias = lax.psum(jnp.stack(bias_grads), ('fsdp', 'seq'))  40.9 us
    reduce_scatter x2, waiting for transfers between devices, per_device(): lax.psum_scatter(mm_nt(g_qkv, w_qkv[l]), 'seq', scatter_dimension=0, tile...  38 us
    all_gather x2, waiting for transfers between devices, per_device(): g_feed_all = lax.all_gather(g_feed, 'seq', axis=0, tiled=True)  36.6 us
  transfers between devices with their start and end apart: 22, of which 16 were waited for; matrix products, arithmetic and copies ran while one was open for 15% of the time, Pallas kernels for 0%

commit v1 on v0

--- a/solution.py
+++ b/solution.py
@@ -247,7 +247,7 @@
     grad_qkv = shared[..., fw + width :].reshape(ns, layers, rows, 3, hc).transpose(1, 2, 3, 0, 4)
     grad_qkv = grad_qkv.reshape(layers, rows, 3 * width)
     grad_out = lax.psum(red[:, :, fw + width : fw + 2 * width], "seq").astype(F32)
-    bias = lax.psum(jnp.stack(bias_grads), ("fsdp", "seq"))
+    bias = jnp.sum(lax.all_gather(jnp.stack(bias_grads), ("fsdp", "seq")), axis=0)
     bias = lax.dynamic_index_in_dim(bias, f, 1, keepdims=False)
     cuts = [qv_bias.shape[1], out_bias.shape[1], up_bias.shape[1], down_bias.shape[1]]
     grad_bias, at = ([], 0)

time: 1020 us -> 1080 us (1.059)
  waiting for transfers between devices: 487 us -> 587 us
  blocking collectives: 203 us -> 152 us
    all_gather x0 -> x1, waiting for transfers between devices: none -> 56.4 us  [per_device(): lax.all_gather(jnp.stack(bias_grads), ('fsdp', 'seq'))]
    psum x1 -> x0, blocking collectives: 40.9 us -> none  [per_device(): bias = lax.psum(jnp.stack(bias_grads), ('fsdp', 'seq'))]
    reduce_scatter x2, waiting for transfers between devices: 38 us -> 74.5 us  [per_device(): lax.psum_scatter(mm_nt(g_qkv, w_qkv[l]), 'seq', scatter_dimension=0, tile...]
    unnamed x22 -> x23, waiting for transfers between devices: 196 us -> 197 us
    unnamed x158 -> x155, local copies, waits for them, and re-layouts: 27.4 us -> 28.7 us
  transfers between devices with their start and end apart: 22 -> 24, of which waited for: 16 -> 19; matrix products, arithmetic and copies ran while one was open for 15% -> 15% of each run, Pallas kernels for 0% -> 0%
where the time goes in v1:
time: 1080 us; the launch traced here: 1070 us
  waiting for transfers between devices  587 us (54%)
  blocking collectives  152 us (14%)
  matrix products  147 us (14%)
  local copies, waits for them, and re-layouts  92.4 us (9%)
  other arithmetic  53.8 us (5%)
  starting transfers between devices  17.4 us (2%)
  between operations  15.9 us (1%)
    unnamed x23, waiting for transfers between devices  197 us
    reduce_scatter x2, waiting for transfers between devices, per_device(): lax.psum_scatter(feed, 'seq', scatter_dimension=0, tiled=True) + down_b[l]  76.8 us
    reduce_scatter x2, waiting for transfers between devices, per_device(): lax.psum_scatter(mm_nt(g_qkv, w_qkv[l]), 'seq', scatter_dimension=0, tile...  74.5 us
    all_gather x2, blocking collectives, per_device(): w_qkv.append(lax.all_gather(q_part, 'fsdp', axis=0, tiled=True))  67.5 us
    all_gather x1, waiting for transfers between devices, per_device(): lax.all_gather(jnp.stack(bias_grads), ('fsdp', 'seq'))  56.4 us
    reduce_scatter x2, waiting for transfers between devices, per_device(): lax.psum_scatter(mm_nt(g_up, w_rest[l][:, :fw]), 'seq', scatter_dimension...  53 us
    all_gather x2, waiting for transfers between devices, per_device(): w_rest.append(lax.all_gather(rest, 'fsdp', axis=0, tiled=True))  43.5 us
    all_gather x2, waiting for transfers between devices, per_device(): g_feed_all = lax.all_gather(g_feed, 'seq', axis=0, tiled=True)  36.6 us
  transfers between devices with their start and end apart: 24, of which 19 were waited for; matrix products, arithmetic and copies ran while one was open for 15% of the time, Pallas kernels for 0%

profile of v1, /device:TPU:0, one launch (start us, length us, event | category | flops | bytes accessed | tf_op | source)
XLA Modules:
  0.0 1065.9 jit_solution(8272478113875984896)
XLA Ops:
  12.4 32.4 %all-gather.3 = bf16[8,1,3456]{2,1,0:T(2,128)(2,1)S(1)} all-gather(bf16[1,1,3456]{2,1,0:T(2,128)(2,1)S(1)} %reshape.392), channel_id=2, replica_groups=mesh['fsdp'=8,'seq'=4] {'fsdp'}, dimensions={0}, use_global_device_ids=true | all-gather | bytes 62208 | tf_op jit(solution)/shard_map/all_gather | solution.py:131
  50.2 71.0 %all-reduce.6.cloned.1.call-done = f32[8,2,4608]{2,1,0:T(2,128)} async-done(((f32[8,2,4608]{2,1,0:T(2,128)}), f32[8,2,4608]{2,1,0:T(2,128)}) %all-reduce.6.cloned.1.call-update) | async-done | bytes 294928
  135.6 34.4 %all_gather.57 = bf16[768,576]{1,0:T(8,128)(2,1)S(1)} all-gather(bf16[96,576]{1,0:T(8,128)(2,1)S(1)} %copy.153), channel_id=1, replica_groups=mesh['fsdp'=8,'seq'=4] {'fsdp'}, dimensions={0}, use_global_device_ids=true | all-gather | bytes 995328 | tf_op jit(solution)/shard_map/all_gather | solution.py:115
  173.0 6.9 fusion.3
  179.9 5.8 fusion.65
  190.8 6.8 all-to-all-done
  197.6 14.9 %all-gather.17.cloned.1.call-done = bf16[768,2304]{1,0:T(8,128)(2,1)} async-done(((bf16[96,2304]{1,0:T(8,128)(2,1)}), bf16[768,2304]{1,0:T(8,128)(2,1)}) %all-gather.17.cloned.1.call-update) | async-done | bytes 3538960 | tf_op jit(solution)/shard_map/all_gather | solution.py:117
  216.7 18.2 %all-gather.19.cloned.1.call-done = bf16[1024,768]{1,0:T(8,128)(2,1)} async-done(((bf16[256,768]{1,0:T(8,128)(2,1)}), bf16[1024,768]{1,0:T(8,128)(2,1)}) %all-gather.19.cloned.1.call-update) | async-done | bytes 1572880 | tf_op jit(solution)/shard_map/all_gather | solution.py:168
  239.7 5.0 fusion.78
  244.9 37.9 %reduce-scatter.13.cloned.1.call-done = f32[256,768]{1,0:T(8,128)} async-done(((f32[1024,768]{1,0:T(8,128)}), f32[256,768]{1,0:T(8,128)}) %reduce-scatter.13.cloned.1.call-update) | async-done | bytes 786448 | tf_op jit(solution)/shard_map/reduce_scatter | solution.py:172
  289.8 33.0 %all_gather.61 = bf16[768,576]{1,0:T(8,128)(2,1)S(1)} all-gather(bf16[96,576]{1,0:T(8,128)(2,1)S(1)} %copy.159), channel_id=1, replica_groups=mesh['fsdp'=8,'seq'=4] {'fsdp'}, dimensions={0}, use_global_device_ids=true | all-gather | bytes 995328 | tf_op jit(solution)/shard_map/all_gather | solution.py:115
  326.4 6.9 fusion.2
  333.3 5.8 fusion.62
  344.0 28.6 %all-gather.23.cloned.1.call-done = bf16[768,2304]{1,0:T(8,128)(2,1)} async-done(((bf16[96,2304]{1,0:T(8,128)(2,1)}), bf16[768,2304]{1,0:T(8,128)(2,1)}) %all-gather.23.cloned.1.call-update) | async-done | bytes 3538960 | tf_op jit(solution)/shard_map/all_gather | solution.py:117
  377.7 17.5 %all-gather.25.cloned.1.call-done = bf16[1024,768]{1,0:T(8,128)(2,1)} async-done(((bf16[256,768]{1,0:T(8,128)(2,1)}), bf16[1024,768]{1,0:T(8,128)(2,1)}) %all-gather.25.cloned.1.call-update) | async-done | bytes 1572880 | tf_op jit(solution)/shard_map/all_gather | solution.py:168
  395.2 4.8 fusion.73
  400.0 17.0 %all-gather.27.cloned.1.call-done = bf16[1024,768]{1,0:T(8,128)(2,1)} async-done(((bf16[256,768]{1,0:T(8,128)(2,1)}), bf16[1024,768]{1,0:T(8,128)(2,1)}) %all-gather.27.cloned.1.call-update) | async-done | bytes 1572880 | tf_op jit(solution)/shard_map/all_gather | solution.py:189
  417.0 5.6 convert_reduce_fusion
  428.2 5.9 fusion.69
  434.2 31.9 %reduce-scatter.17.cloned.1.call-done = f32[256,768]{1,0:T(8,128)} async-done(((f32[1024,768]{1,0:T(8,128)}), f32[256,768]{1,0:T(8,128)}) %reduce-scatter.17.cloned.1.call-update) | async-done | bytes 786448 | tf_op jit(solution)/shard_map/reduce_scatter | solution.py:193
  467.7 38.9 %reduce-scatter.15.cloned.1.call-done = f32[256,768]{1,0:T(8,128)} async-done(((f32[1024,768]{1,0:T(8,128)}), f32[256,768]{1,0:T(8,128)}) %reduce-scatter.15.cloned.1.call-update) | async-done | bytes 786448 | tf_op jit(solution)/shard_map/reduce_scatter | solution.py:172
  511.6 10.2 all_to_all.80
  523.1 7.5 convert_reduce_fusion.5
  530.6 6.8 multiply_reduce_fusion.1
  537.9 5.2 multiply_convert_fusion.1
  543.2 5.0 fusion.46
  553.5 38.0 %reduce-scatter.19.cloned.1.call-done = f32[256,768]{1,0:T(8,128)} async-done(((f32[1024,768]{1,0:T(8,128)}), f32[256,768]{1,0:T(8,128)}) %reduce-scatter.19.cloned.1.call-update) | async-done | bytes 786448 | tf_op jit(solution)/shard_map/reduce_scatter | solution.py:207
  595.6 19.6 %all-gather.29.cloned.1.call-done = bf16[1024,768]{1,0:T(8,128)(2,1)} async-done(((bf16[256,768]{1,0:T(8,128)(2,1)}), bf16[1024,768]{1,0:T(8,128)(2,1)}) %all-gather.29.cloned.1.call-update) | async-done | bytes 1572880 | tf_op jit(solution)/shard_map/all_gather | solution.py:189
  615.2 5.6 convert_reduce_fusion.1
  621.9 4.4 fusion.80
  636.8 6.5 copy.190
  643.4 21.0 %reduce-scatter.21.cloned.1.call-done = f32[256,768]{1,0:T(8,128)} async-done(((f32[1024,768]{1,0:T(8,128)}), f32[256,768]{1,0:T(8,128)}) %reduce-scatter.21.cloned.1.call-update) | async-done | bytes 786448 | tf_op jit(solution)/shard_map/reduce_scatter | solution.py:193
  675.9 6.1 all-to-all-done.3
  682.5 6.8 convert_reduce_fusion.9
  689.4 6.6 multiply_reduce_fusion
  696.1 6.8 multiply_convert_fusion
  706.5 4.9 fusion.47
  724.6 6.5 copy.188
  731.3 30.2 %reduce-scatter.27.cloned.1.call-done = bf16[96,2880]{1,0:T(8,128)(2,1)} async-done(((bf16[768,2880]{1,0:T(8,128)(2,1)}), bf16[96,2880]{1,0:T(8,128)(2,1)}) %reduce-scatter.27.cloned.1.call-update) | async-done | bytes 552976
  762.9 56.4 %all-gather.33.cloned.1.call-done = f32[64,8,768]{2,1,0:T(8,128)} async-done(((f32[2,8,768]{2,1,0:T(8,128)}), f32[64,8,768]{2,1,0:T(8,128)}) %all-gather.33.cloned.1.call-update) | async-done | bytes 1572880 | tf_op jit(solution)/shard_map/all_gather | solution.py:250
  822.6 36.5 %reduce-scatter.23.cloned.1.call-done = f32[256,768]{1,0:T(8,128)} async-done(((f32[1024,768]{1,0:T(8,128)}), f32[256,768]{1,0:T(8,128)}) %reduce-scatter.23.cloned.1.call-update) | async-done | bytes 786448 | tf_op jit(solution)/shard_map/reduce_scatter | solution.py:207
  860.7 95.8 %reduce-scatter.25.cloned.1.call-done = bf16[96,2880]{1,0:T(8,128)(2,1)} async-done(((bf16[768,2880]{1,0:T(8,128)(2,1)}), bf16[96,2880]{1,0:T(8,128)(2,1)}) %reduce-scatter.25.cloned.1.call-update) | async-done | bytes 552976
  965.3 11.1 %psum.14 = f32[1,2,4608]{2,1,0:T(2,128)S(1)} all-reduce(f32[1,2,4608]{2,1,0:T(2,128)S(1)} %maximum_bitcast_fusion), channel_id=1, replica_groups=mesh['fsdp'=8,'seq'=4] {'seq'}, use_global_device_ids=true, to_apply=%region_39.40 | all-reduce | flops 9216 | bytes 73728 | tf_op jit(solution)/shard_map/psum | solution.py:257
  976.3 31.0 %all_gather.67 = f32[8,2,4608]{2,1,0:T(2,128)S(1)} all-gather(f32[1,2,4608]{2,1,0:T(2,128)S(1)} %psum.14), channel_id=1, replica_groups=mesh['fsdp'=8,'seq'=4] {'fsdp'}, dimensions={0}, use_global_device_ids=true | all-gather | bytes 331776 | tf_op jit(solution)/shard_map/all_gather | solution.py:258
  1009.9 5.2 all-to-all-start.4
  1025.4 6.8 copy.175
  1035.5 5.1 slice_bitcast_fusion
  1047.1 5.3 reshape.377
  (397 shorter events, 169.8 us)
Async XLA Ops:
  7.2 42.1 %copy-start.57 = (u32[32]{0:T(128)S(1)}, u32[32]{0:T(128)}, u32[]{:S(2)}) copy-start(u32[32]{0:T(128)} %constant.102) | copy-start | bytes 388
  7.2 41.7 %copy-start.4 = (bf16[1,256,768]{2,1,0:T(8,128)(2,1)S(1)}, bf16[1,256,768]{2,1,0:T(8,128)(2,1)}, u32[]{:S(2)}) copy-start(bf16[1,256,768]{2,1,0:T(8,128)(2,1)} %param.13) | copy-start | bytes 1179652
  7.2 113.9 %all-reduce.6.cloned.1.call-start = ((), (), s32[]{:S(2)}) async-start(), calls=%async_computation.32 | async-start | bytes 589824
  44.8 79.0 %copy-start.30 = (bf16[2,96,3072]{2,1,0:T(8,128)(2,1)S(1)}, bf16[2,96,3072]{2,1,0:T(8,128)(2,1)}, u32[]{:S(2)}) copy-start(bf16[2,96,3072]{2,1,0:T(8,128)(2,1)} %param.21) | copy-start | bytes 3538948
  44.9 76.3 %copy-start.45 = (bf16[8,768]{1,0:T(8,128)(2,1)}, bf16[8,768]{1,0:T(8,128)(2,1)S(1)}, u32[]{:S(2)}) copy-start(bf16[8,768]{1,0:T(8,128)(2,1)S(1)} %get-tuple-element.176) | copy-start | bytes 36868
  48.8 121.1 %all-gather.15.cloned.1.call-start = ((), (), s32[]{:S(2)}) async-start(), calls=%async_computation.13 | async-start | bytes 1966080 | tf_op jit(solution)/shard_map/all_gather | solution.py:159
  49.1 76.8 %copy-start.46 = (f32[256]{0:T(256)}, f32[256]{0:T(256)S(1)}, u32[]{:S(2)}) copy-start(f32[256]{0:T(256)S(1)} %broadcast_multiply_fusion.11) | copy-start | bytes 3076
  50.1 78.1 %copy-start.48 = (f32[256]{0:T(256)}, f32[256]{0:T(256)S(1)}, u32[]{:S(2)}) copy-start(f32[256]{0:T(256)S(1)} %add_rsqrt_fusion.3) | copy-start | bytes 3076
  123.7 88.8 %all-gather.17.cloned.1.call-start = ((), (), s32[]{:S(2)}) async-start(), calls=%async_computation.14 | async-start | bytes 3981312 | tf_op jit(solution)/shard_map/all_gather | solution.py:117
  173.0 6.9 copy-start.20
  186.8 10.8 %all-to-all-start = ((bf16[4,256,192]{1,2,0:T(8,128)(2,1)}), bf16[4,256,192]{1,2,0:T(8,128)(2,1)S(1)}, u32[]{:S(2)}, u32[]{:S(2)}) async-start(bf16[4,256,192]{1,2,0:T(8,128)(2,1)} %copy.156), calls=%async_computation | async-start | bytes 786432 | tf_op jit(solution)/shard_map/all_to_all | solution.py:163
  190.2 44.7 %all-gather.19.cloned.1.call-start = ((), (), s32[]{:S(2)}) async-start(), calls=%async_computation.15 | async-start | bytes 1966080 | tf_op jit(solution)/shard_map/all_gather | solution.py:168
  197.6 40.5 %copy-start.14 = (bf16[4,256,192]{1,2,0:T(8,128)(2,1)}, bf16[4,256,192]{1,2,0:T(8,128)(2,1)S(1)}, u32[]{:S(2)}) copy-start(bf16[4,256,192]{1,2,0:T(8,128)(2,1)S(1)} %all-to-all-done) | copy-start | bytes 1179652
  215.2 67.6 %copy-start.2 = (f32[256,768]{1,0:T(8,128)}, f32[256,768]{1,0:T(8,128)S(1)}, u32[]{:S(2)}) copy-start(f32[256,768]{1,0:T(8,128)S(1)} %get-tuple-element.143) | copy-start | bytes 2359300
  216.4 66.4 %reduce-scatter.13.cloned.1.call-start = ((), (), s32[]{:S(2)}) async-start(), calls=%async_computation.16 | async-start | bytes 3932160 | tf_op jit(solution)/shard_map/reduce_scatter | solution.py:172
  244.8 78.1 %all-gather.21.cloned.1.call-start = ((), (), s32[]{:S(2)}) async-start(), calls=%async_computation.17 | async-start | bytes 1966080 | tf_op jit(solution)/shard_map/all_gather | solution.py:159
  285.4 87.2 %all-gather.23.cloned.1.call-start = ((), (), s32[]{:S(2)}) async-start(), calls=%async_computation.18 | async-start | bytes 3981312 | tf_op jit(solution)/shard_map/all_gather | solution.py:117
  326.4 6.9 copy-start.22
  326.4 6.9 copy-start.28
  326.4 6.9 copy-start.10
  340.2 32.4 %all-to-all-start.1 = ((bf16[4,256,192]{1,2,0:T(8,128)(2,1)}), bf16[4,256,192]{1,2,0:T(8,128)(2,1)S(1)}, u32[]{:S(2)}, u32[]{:S(2)}) async-start(bf16[4,256,192]{1,2,0:T(8,128)(2,1)} %copy.161), calls=%async_computation.2 | async-start | bytes 786432 | tf_op jit(solution)/shard_map/all_to_all | solution.py:163
  343.6 51.5 %all-gather.25.cloned.1.call-start = ((), (), s32[]{:S(2)}) async-start(), calls=%async_computation.19 | async-start | bytes 1966080 | tf_op jit(solution)/shard_map/all_gather | solution.py:168
  376.7 40.3 %all-gather.27.cloned.1.call-start = ((), (), s32[]{:S(2)}) async-start(), calls=%async_computation.21 | async-start | bytes 1966080 | tf_op jit(solution)/shard_map/all_gather | solution.py:189
  377.6 88.6 %reduce-scatter.17.cloned.1.call-start = ((), (), s32[]{:S(2)}) async-start(), calls=%async_computation.22 | async-start | bytes 3932160 | tf_op jit(solution)/shard_map/reduce_scatter | solution.py:193
  428.1 78.5 %reduce-scatter.15.cloned.1.call-start = ((), (), s32[]{:S(2)}) async-start(), calls=%async_computation.20 | async-start | bytes 3932160 | tf_op jit(solution)/shard_map/reduce_scatter | solution.py:172
  434.1 157.4 %reduce-scatter.19.cloned.1.call-start = ((), (), s32[]{:S(2)}) async-start(), calls=%async_computation.23 | async-start | bytes 3932160 | tf_op jit(solution)/shard_map/reduce_scatter | solution.py:207
  509.5 12.3 %copy-start.24 = (bf16[256,768]{1,0:T(8,128)(2,1)}, bf16[256,768]{1,0:T(8,128)(2,1)S(1)}, u32[]{:S(2)}) copy-start(bf16[256,768]{1,0:T(8,128)(2,1)S(1)} %get-tuple-element.163) | copy-start | bytes 1179652
  523.1 14.3 %slice-start = ((s8[12582912]{0:T(1024)(128)(4,1)}), s8[4194304]{0:T(1024)(128)(4,1)S(1)}, s32[]{:S(2)}) async-start(s8[12582912]{0:T(1024)(128)(4,1)} %bitcast.263), calls=%async_computation.33 | async-start | bytes 8388608
  530.6 7.3 slice-start.2
  553.4 39.6 %copy-start.16 = (f32[256,768]{1,0:T(8,128)S(1)}, f32[256,768]{1,0:T(8,128)}, u32[]{:S(2)}) copy-start(f32[256,768]{1,0:T(8,128)} %get-tuple-element.164) | copy-start | bytes 2359300
  553.4 39.6 %copy-start.17 = (f32[256,768]{1,0:T(8,128)S(1)}, f32[256,768]{1,0:T(8,128)}, u32[]{:S(2)}) copy-start(f32[256,768]{1,0:T(8,128)} %get-tuple-element.182) | copy-start | bytes 2359300
  553.5 61.7 %all-gather.29.cloned.1.call-start = ((), (), s32[]{:S(2)}) async-start(), calls=%async_computation.24 | async-start | bytes 1966080 | tf_op jit(solution)/shard_map/all_gather | solution.py:189
  595.4 69.0 %reduce-scatter.21.cloned.1.call-start = ((), (), s32[]{:S(2)}) async-start(), calls=%async_computation.25 | async-start | bytes 3932160 | tf_op jit(solution)/shard_map/reduce_scatter | solution.py:193
  626.4 135.1 %reduce-scatter.27.cloned.1.call-start = ((), (), s32[]{:S(2)}) async-start(), calls=%async_computation.31 | async-start | bytes 5087232
  643.4 21.1 %copy-start.3 = (f32[256,768]{1,0:T(8,128)S(1)}, f32[256,768]{1,0:T(8,128)}, u32[]{:S(2)}) copy-start(f32[256,768]{1,0:T(8,128)} %copy-done.2) | copy-start | bytes 2359300
  643.4 22.6 %copy-start.19 = (f32[256,768]{1,0:T(8,128)S(1)}, f32[256,768]{1,0:T(8,128)}, u32[]{:S(2)}) copy-start(f32[256,768]{1,0:T(8,128)} %reduce-scatter.13.cloned.1.call-done) | copy-start | bytes 2359300
  671.1 10.8 %all-to-all-start.3 = ((bf16[256,4,192]{0,2,1:T(8,128)(2,1)}), bf16[256,4,192]{0,2,1:T(8,128)(2,1)S(1)}, u32[]{:S(2)}, u32[]{:S(2)}) async-start(bf16[256,4,192]{0,2,1:T(8,128)(2,1)} %bitcast.53), calls=%async_computation.8 | async-start | bytes 786432 | tf_op jit(solution)/shard_map/all_to_all | solution.py:203
  674.6 144.7 %all-gather.33.cloned.1.call-start = ((), (), s32[]{:S(2)}) async-start(), calls=%async_computation.29 | async-start | bytes 1622016 | tf_op jit(solution)/shard_map/all_gather | solution.py:250
  706.5 152.6 %reduce-scatter.23.cloned.1.call-start = ((), (), s32[]{:S(2)}) async-start(), calls=%async_computation.26 | async-start | bytes 3932160 | tf_op jit(solution)/shard_map/reduce_scatter | solution.py:207
  714.6 241.9 %reduce-scatter.25.cloned.1.call-start = ((), (), s32[]{:S(2)}) async-start(), calls=%async_computation.30 | async-start | bytes 5087232
  731.1 128.0 %copy-start.5 = (bf16[1,256,768]{2,1,0:T(8,128)(2,1)S(1)}, bf16[1,256,768]{2,1,0:T(8,128)(2,1)}, u32[]{:S(2)}) copy-start(bf16[1,256,768]{2,1,0:T(8,128)(2,1)} %param.13) | copy-start | bytes 1179652
  731.1 128.0 %copy-start.44 = (f32[768]{0:T(1024)S(1)}, f32[768]{0:T(1024)}, u32[]{:S(2)}) copy-start(f32[768]{0:T(1024)} %copy-done.43) | copy-start | bytes 9220
  731.1 128.0 %copy-start.47 = (f32[256]{0:T(256)S(1)}, f32[256]{0:T(256)}, u32[]{:S(2)}) copy-start(f32[256]{0:T(256)} %copy-done.46) | copy-start | bytes 3076
  731.1 128.0 %copy-start.49 = (f32[256]{0:T(256)S(1)}, f32[256]{0:T(256)}, u32[]{:S(2)}) copy-start(f32[256]{0:T(256)} %copy-done.48) | copy-start | bytes 3076
  731.1 292.3 %all-reduce.4.cloned.1.call-start = ((), (), s32[]{:S(2)}) async-start(), calls=%async_computation.27 | async-start | bytes 786432 | tf_op jit(solution)/shard_map/psum | solution.py:249
  959.8 65.6 %all-gather.31.cloned.1.call-start = ((), (), s32[]{:S(2)}) async-start(), calls=%async_computation.28 | async-start | bytes 4177920 | tf_op jit(solution)/shard_map/all_gather | solution.py:239
  962.4 45.3 %copy-start.7 = (bf16[2,96,4608]{2,1,0:T(8,128)(2,1)S(1)}, bf16[2,96,4608]{2,1,0:T(8,128)(2,1)}, u32[]{:S(2)}) copy-start(bf16[2,96,4608]{2,1,0:T(8,128)(2,1)} %param.15) | copy-start | bytes 5308420
  1009.9 11.6 %all-to-all-start.4 = ((f32[8,1,96]{2,1,0:T(1,128)}), f32[8,1,96]{2,1,0:T(1,128)S(1)}, u32[]{:S(2)}, u32[]{:S(2)}) async-start(f32[8,1,96]{2,1,0:T(1,128)} %bitcast.68), calls=%async_computation.10 | async-start | bytes 8192 | tf_op jit(solution)/shard_map/all_to_all | solution.py:285
  (42 other events, 143.6 us)
Sparse Core Ops, SparseCore 0:
  49.0 72.1 all-reduce.5
  123.8 18.6 all-gather.14
  145.3 67.1 all-gather.16
  216.5 18.3 all-gather.18
  244.9 37.8 reduce-scatter.12
  285.5 19.6 all-gather.20
  307.9 64.5 all-gather.22
  376.8 18.3 all-gather.24
  397.3 19.6 all-gather.26
  428.2 37.8 reduce-scatter.16
  468.7 37.8 reduce-scatter.14
  553.6 37.8 reduce-scatter.18
  595.5 19.6 all-gather.28
  626.5 37.8 reduce-scatter.20
  667.9 93.5 reduce-scatter.26
  764.7 54.4 all-gather.32
  822.2 36.8 reduce-scatter.22
  862.6 93.8 reduce-scatter.24
  959.9 32.6 all-reduce.3
  994.5 29.6 all-gather.30
